TPU v7x, 32 devices: a whole 2x2x4 slice. The times are simulated.
32 devices in a mesh: leaf: 16 (over z, y, x), player: 2 (over core).
Axes of the slice: x: 2, y: 2, z: 4, core: 2. Of those that a mesh axis runs over, the one named last changes fastest.
Arguments:
- chance_reach: float32 [2, 512, 1326], P('player', 'leaf'), may hold values from 0.02 to 1
- regrets_start: float32 [2, 512, 1326], P('player', 'leaf'), may hold values from -6 to 6
- pot: float32 [512], P('leaf'), may hold values from 1 to 8
- parent: int32 [2, 512], P('player'), may hold values from 0 to 255, never falling along the last dimension, each value on 1 to 6 neighbouring positions
- hand_cards: int32 [1326, 2], replicated, may hold values from 0 to 51, as said below
- board_cards: int32 [64, 5], P('leaf'), may hold values from 0 to 51, as said below
- hand_rank: int32 [64, 1326], P('leaf'), may hold values from 0 to 1999
Outputs:
- regrets: float32 [2, 512, 1326], P('player', 'leaf')
- values: float32 [2, 512, 1326], P('player', 'leaf')
Inputs may be any that keep to these rules, and one draw needn't show every extreme that they name: `parent`: along each row the node ids never fall; each node owns 1 to 6 consecutive leaves, one exactly 6; every id up to 255 occurs. `hand_cards`: distinct pairs of two different cards, the smaller card first. `board_cards`: five different cards on each board.
All inputs are finite; a program needn't handle non-finite values.
Results may differ from a plain program's by a relative error of at most 0.0003.
Values sent between devices are 32-bit elements; how exact they have to be, the bound alone decides.
A program may use at most 128 MiB of HBM per device.

v0:
```python
import jax
import jax.numpy as jnp
from jax import lax
from jax.sharding import PartitionSpec as P

ITERS = 2


DELTA = 0.05
EPSILON = 1e-06
DECK_SIZE = 52


def extended(array, sides, width):
    for axis, dim in sides:
        size, length = (lax.axis_size(axis), array.shape[dim])
        up = [(i, (i + 1) % size) for i in range(size - 1)]
        down = [(j, i) for i, j in up]
        last = lax.slice_in_dim(array, length - width, length, axis=dim)
        first = lax.slice_in_dim(array, 0, width, axis=dim)
        before = lax.ppermute(last, axis, up)
        after = lax.ppermute(first, axis, down)
        array = jnp.concatenate([before, array, after], axis=dim)
    return array


def partner(array, axis, stride):
    return lax.ppermute(array, axis, [(i, i ^ 1 << stride) for i in range(lax.axis_size(axis))])


def holding_table(hand_cards):
    deck_cards = jnp.arange(DECK_SIZE, dtype=jnp.int32)
    holding = (hand_cards[:, 0:1] == deck_cards[None, :]) | (
        hand_cards[:, 1:2] == deck_cards[None, :]
    )
    return holding.astype(jnp.float32)


def board_free(board_cards, holding):
    deck_cards = jnp.arange(DECK_SIZE, dtype=jnp.int32)
    on_board = jnp.any(board_cards[:, :, None] == deck_cards[None, None, :], axis=1).astype(
        jnp.float32
    )
    touched = jnp.dot(on_board, holding.T, precision=lax.Precision.HIGHEST)
    return (touched < 0.5).astype(jnp.float32)


def payoff_matrix(rank_row, free_row, apart_mask):
    ranked = rank_row.astype(jnp.float32)
    sign_table = jnp.sign(ranked[:, None] - ranked[None, :])
    return sign_table * apart_mask * free_row[:, None] * free_row[None, :]


def showdown(opposed, pot, matrices):
    board_count = matrices.shape[0]
    hand_count = opposed.shape[1]
    blocks = opposed.reshape(board_count, -1, hand_count)
    pot_rows = pot.reshape(board_count, -1)

    def one_board(board_items):
        matrix, opp_block, pot_row = board_items
        summed = jnp.dot(opp_block, matrix.T, precision=lax.Precision.HIGHEST)
        return summed * (pot_row[:, None] * (1.0 / hand_count))

    return lax.map(one_board, (matrices, blocks, pot_rows)).reshape(opposed.shape)


def local(chance_reach, regrets_start, pot, parent, hand_cards, board_cards, hand_rank):
    chance = chance_reach[0]
    regrets = regrets_start[0]
    parents = parent[0]
    leaf_rows = chance.shape[0]
    hand_count = chance.shape[1]
    leaf_count = parents.shape[0]
    holding = holding_table(hand_cards)
    apart_mask = (jnp.dot(holding, holding.T, precision=lax.Precision.HIGHEST) < 0.5).astype(
        jnp.float32
    )
    free_rows = board_free(board_cards, holding)
    matrices = lax.map(
        lambda items: payoff_matrix(items[0], items[1], apart_mask), (hand_rank, free_rows)
    )
    first_leaf = lax.axis_index("leaf") * leaf_rows
    local_parent = lax.dynamic_slice_in_dim(parents, first_leaf, leaf_rows)
    local_ids = local_parent - local_parent[0]
    last_id = local_ids[leaf_rows - 1]
    before_id = parents[jnp.maximum(first_leaf - 1, 0)]
    after_id = parents[jnp.minimum(first_leaf + leaf_rows, leaf_count - 1)]
    joins_before = (first_leaf > 0) & (before_id == local_parent[0])
    joins_after = (first_leaf + leaf_rows < leaf_count) & (after_id == local_parent[leaf_rows - 1])

    def node_totals(values):
        segment_sums = jax.ops.segment_sum(values, local_ids, num_segments=leaf_rows)
        edge_sums = jnp.stack([segment_sums[0], segment_sums[last_id]])
        padded = extended(edge_sums, (("leaf", 0),), 1)
        segment_sums = segment_sums.at[0].add(jnp.where(joins_before, padded[0], 0.0))
        segment_sums = segment_sums.at[last_id].add(jnp.where(joins_after, padded[3], 0.0))
        return segment_sums[local_ids]

    values = jnp.zeros((leaf_rows, hand_count), jnp.float32)
    for iteration in range(ITERS):
        positive = jnp.maximum(regrets, 0.0) + DELTA
        policy = positive / node_totals(positive)
        own_reach = chance * policy
        opposed = partner(own_reach, "player", 0)
        values = showdown(opposed, pot, matrices)
        instant = values - node_totals(policy * values)
        squares = lax.psum(jnp.sum(instant * instant), "leaf")
        norm_scale = jnp.sqrt(squares / (leaf_count * hand_count) + EPSILON)
        regrets = regrets + instant / norm_scale
    return (regrets[None], values[None])


def solution(mesh):
    in_specs = (
        P("player", "leaf", None),
        P("player", "leaf", None),
        P("leaf"),
        P("player", None),
        P(),
        P("leaf", None),
        P("leaf", None),
    )
    out_specs = (P("player", "leaf", None), P("player", "leaf", None))
    return jax.shard_map(local, mesh=mesh, in_specs=in_specs, out_specs=out_specs, check_vma=False)
```

profile of v0, /device:TPU:0, one launch (start us, length us, event | category | flops | bytes accessed | tf_op | source)
XLA Modules:
  0.0 257.2 jit_solution(8346592243326083595)
XLA Ops:
  0.6 0.7 constant_dynamic-slice_fusion.8
  1.9 1.4 fusion.74
  6.1 1.3 scatter_custom_fusion
  7.4 4.9 %collective-permute-start = (f32[1,1326]{1,0:T(1,128)S(1)}, f32[1,1326]{1,0:T(1,128)S(1)}, u32[]{:S(2)}, u32[]{:S(2)}) collective-permute-start(f32[1,1326]{1,0:T(1,128)S(1)} %constant_dynamic-slice_fusion.6), channel_id=1, source_target_pairs={{0,2},{2,4},{4,6},{6,8},{8,10},{10,12},{12,14},{14,16},{16,18},{18... | collective-permute-start | bytes 15920 | tf_op jit(solution)/shard_map/ppermute | solution.py:21
  12.3 0.8 slice_reduce_fusion.1
  13.1 0.8 copy.9
  14.0 4.5 %fusion.37 = f32[1326,1326]{1,0:T(8,128)} fusion(s32[1326]{0:T(1024)S(1)} %get-tuple-element.183, s32[1326]{0:T(1024)S(1)} %get-tuple-element.182), kind=kOutput, calls=%fused_computation.39 | convolution fusion | flops 186584096 | bytes 7043712 | tf_op jit(solution)/shard_map/dot_general | solution.py:76
  19.0 0.7 and_reduce_fusion
  21.7 1.3 collective-permute-start.1
  24.4 2.7 %collective-permute-done.1 = f32[1,1326]{1,0:T(1,128)S(1)} collective-permute-done((f32[1,1326]{1,0:T(1,128)S(1)}, f32[1,1326]{1,0:T(1,128)S(1)}, u32[]{:S(2)}, u32[]{:S(2)}) %collective-permute-start.1) | collective-permute-done | bytes 5336 | tf_op jit(solution)/shard_map/ppermute | solution.py:22
  28.7 30.6 %while.38 = (s32[]{:T(128)}, f32[4,1326,1326]{2,1,0:T(8,128)}, s32[4,1326]{1,0:T(4,128)}, f32[1326,1326]{1,0:T(8,128)}, f32[4,1326]{1,0:T(4,128)S(1)}, /*index=5*/s32[]{:T(128)}) while((s32[]{:T(128)}, f32[4,1326,1326]{2,1,0:T(8,128)}, s32[4,1326]{1,0:T(4,128)}, f32[1326,1326]{1,0:T(8,128)}, f32[4,1326]{1,0:T(4,128)S(1)}, ...), condition=%wide.region_2.3_spmd, body=%wide.region_1.2_spmd.sunk | while | flops 8792708 | bytes 15013161 | solution.py:80
  28.7 0.8 dynamic-slice_reduce_fusion.2
  29.5 6.8 %fusion.91 = f32[4,1326,1326]{2,1,0:T(8,128)} fusion(f32[4,1326,1326]{2,1,0:T(8,128)} %get-tuple-element.336, s32[]{:T(128)} %get-tuple-element.335, f32[1326,1326]{1,0:T(8,128)} %get-tuple-element.344, f32[1326]{0:T(1024)S(1)} %get-tuple-element.317, f32[1326]{0:T(1024)S(1)} %get-tuple-element.318), kind=kLoop, calls=%fused_computation.35.clone.1 | loop fusion | flops 8791380 | bytes 14991872 | tf_op jit(solution)/shard_map/while/body/jit(dynamic_update_index_in_dim)/dynamic_update_slice | solution.py:80
  36.3 0.8 dynamic-slice_reduce_fusion.2
  37.1 6.9 %fusion.91 = f32[4,1326,1326]{2,1,0:T(8,128)} fusion(f32[4,1326,1326]{2,1,0:T(8,128)} %get-tuple-element.336, s32[]{:T(128)} %get-tuple-element.335, f32[1326,1326]{1,0:T(8,128)} %get-tuple-element.344, f32[1326]{0:T(1024)S(1)} %get-tuple-element.317, f32[1326]{0:T(1024)S(1)} %get-tuple-element.318), kind=kLoop, calls=%fused_computation.35.clone.1 | loop fusion | flops 8791380 | bytes 14991872 | tf_op jit(solution)/shard_map/while/body/jit(dynamic_update_index_in_dim)/dynamic_update_slice | solution.py:80
  44.0 0.8 dynamic-slice_reduce_fusion.2
  44.8 6.9 %fusion.91 = f32[4,1326,1326]{2,1,0:T(8,128)} fusion(f32[4,1326,1326]{2,1,0:T(8,128)} %get-tuple-element.336, s32[]{:T(128)} %get-tuple-element.335, f32[1326,1326]{1,0:T(8,128)} %get-tuple-element.344, f32[1326]{0:T(1024)S(1)} %get-tuple-element.317, f32[1326]{0:T(1024)S(1)} %get-tuple-element.318), kind=kLoop, calls=%fused_computation.35.clone.1 | loop fusion | flops 8791380 | bytes 14991872 | tf_op jit(solution)/shard_map/while/body/jit(dynamic_update_index_in_dim)/dynamic_update_slice | solution.py:80
  51.7 0.8 dynamic-slice_reduce_fusion.2
  52.5 6.8 %fusion.91 = f32[4,1326,1326]{2,1,0:T(8,128)} fusion(f32[4,1326,1326]{2,1,0:T(8,128)} %get-tuple-element.336, s32[]{:T(128)} %get-tuple-element.335, f32[1326,1326]{1,0:T(8,128)} %get-tuple-element.344, f32[1326]{0:T(1024)S(1)} %get-tuple-element.317, f32[1326]{0:T(1024)S(1)} %get-tuple-element.318), kind=kLoop, calls=%fused_computation.35.clone.1 | loop fusion | flops 8791380 | bytes 14991872 | tf_op jit(solution)/shard_map/while/body/jit(dynamic_update_index_in_dim)/dynamic_update_slice | solution.py:80
  59.4 36.1 %while.39 = (s32[]{:T(128)}, f32[4,8,1326]{2,1,0:T(8,128)S(1)}, f32[4,8,1326]{2,1,0:T(8,128)S(1)}, f32[4,1326,1326]{2,1,0:T(8,128)}, f32[4,8]{1,0:T(4,128)S(1)}, /*index=5*/s32[]{:T(128)}) while((s32[]{:T(128)}, f32[4,8,1326]{2,1,0:T(8,128)S(1)}, f32[4,8,1326]{2,1,0:T(8,128)S(1)}, f32[4,1326,1326]{2,1,0:T(8,128)}, f32[4,8]{1,0:T(4,128)S(1)}, ...), condition=%wide.region_6.7_spmd, body=%wide.region_5.6_spmd.sunk | while | flops 168805120 | bytes 7571593 | solution.py:65
  59.4 9.0 %fusion.95 = f32[4,8,1326]{2,1,0:T(8,128)S(1)} fusion(f32[4,8,1326]{2,1,0:T(8,128)S(1)} %get-tuple-element.354, s32[]{:T(128)} %get-tuple-element.353, f32[4,1326,1326]{2,1,0:T(8,128)} %get-tuple-element.362, f32[4,8,1326]{2,1,0:T(8,128)S(1)} %get-tuple-element.361, f32[8]{0:T(128)S(1)} %fusion.94), kind=kOutput, calls=%fused_computation.13.clone.1 | convolution fusion | flops 168805104 | bytes 7571456 | tf_op jit(solution)/shard_map/while/body/eval_jaxpr/dot_general | solution.py:62
  68.5 9.0 %fusion.95 = f32[4,8,1326]{2,1,0:T(8,128)S(1)} fusion(f32[4,8,1326]{2,1,0:T(8,128)S(1)} %get-tuple-element.354, s32[]{:T(128)} %get-tuple-element.353, f32[4,1326,1326]{2,1,0:T(8,128)} %get-tuple-element.362, f32[4,8,1326]{2,1,0:T(8,128)S(1)} %get-tuple-element.361, f32[8]{0:T(128)S(1)} %fusion.94), kind=kOutput, calls=%fused_computation.13.clone.1 | convolution fusion | flops 168805104 | bytes 7571456 | tf_op jit(solution)/shard_map/while/body/eval_jaxpr/dot_general | solution.py:62
  77.5 9.0 %fusion.95 = f32[4,8,1326]{2,1,0:T(8,128)S(1)} fusion(f32[4,8,1326]{2,1,0:T(8,128)S(1)} %get-tuple-element.354, s32[]{:T(128)} %get-tuple-element.353, f32[4,1326,1326]{2,1,0:T(8,128)} %get-tuple-element.362, f32[4,8,1326]{2,1,0:T(8,128)S(1)} %get-tuple-element.361, f32[8]{0:T(128)S(1)} %fusion.94), kind=kOutput, calls=%fused_computation.13.clone.1 | convolution fusion | flops 168805104 | bytes 7571456 | tf_op jit(solution)/shard_map/while/body/eval_jaxpr/dot_general | solution.py:62
  86.5 9.0 %fusion.95 = f32[4,8,1326]{2,1,0:T(8,128)S(1)} fusion(f32[4,8,1326]{2,1,0:T(8,128)S(1)} %get-tuple-element.354, s32[]{:T(128)} %get-tuple-element.353, f32[4,1326,1326]{2,1,0:T(8,128)} %get-tuple-element.362, f32[4,8,1326]{2,1,0:T(8,128)S(1)} %get-tuple-element.361, f32[8]{0:T(128)S(1)} %fusion.94), kind=kOutput, calls=%fused_computation.13.clone.1 | convolution fusion | flops 168805104 | bytes 7571456 | tf_op jit(solution)/shard_map/while/body/eval_jaxpr/dot_general | solution.py:62
  95.5 1.0 scatter_custom_fusion.1
  96.5 4.3 %collective-permute-start.3 = (f32[1,1326]{1,0:T(1,128)S(1)}, f32[1,1326]{1,0:T(1,128)S(1)}, u32[]{:S(2)}, u32[]{:S(2)}) collective-permute-start(f32[1,1326]{1,0:T(1,128)S(1)} %constant_dynamic-slice_fusion.4), channel_id=1, source_target_pairs={{0,2},{2,4},{4,6},{6,8},{8,10},{10,12},{12,14},{14,16},{16,18},{18... | collective-permute-start | bytes 15920 | tf_op jit(solution)/shard_map/ppermute | solution.py:21
  100.8 1.3 collective-permute-done.3
  102.1 1.3 collective-permute-start.4
  103.6 4.3 %collective-permute-done.4 = f32[1,1326]{1,0:T(1,128)S(1)} collective-permute-done((f32[1,1326]{1,0:T(1,128)S(1)}, f32[1,1326]{1,0:T(1,128)S(1)}, u32[]{:S(2)}, u32[]{:S(2)}) %collective-permute-start.4) | collective-permute-done | bytes 5336 | tf_op jit(solution)/shard_map/ppermute | solution.py:22
  110.0 41.4 %psum.14 = f32[]{:T(128)} all-reduce(f32[]{:T(128)} %fusion.52), channel_id=1, replica_groups=mesh['leaf'=16,'player'=2] {'leaf'}, use_global_device_ids=true, to_apply=%region_9.10 | all-reduce | flops 1 | bytes 8 | tf_op jit(solution)/shard_map/psum | solution.py:108
  152.1 0.9 scatter_custom_fusion.2
  153.1 1.3 collective-permute-start.5
  154.4 1.3 collective-permute-done.5
  155.7 1.3 collective-permute-start.6
  157.2 4.3 %collective-permute-done.6 = f32[1,1326]{1,0:T(1,128)S(1)} collective-permute-done((f32[1,1326]{1,0:T(1,128)S(1)}, f32[1,1326]{1,0:T(1,128)S(1)}, u32[]{:S(2)}, u32[]{:S(2)}) %collective-permute-start.6) | collective-permute-done | bytes 5336 | tf_op jit(solution)/shard_map/ppermute | solution.py:22
  163.2 1.4 collective-permute-done.7
  164.6 36.1 %while.40 = (s32[]{:T(128)}, f32[4,8,1326]{2,1,0:T(8,128)S(1)}, f32[4,8,1326]{2,1,0:T(8,128)S(1)}, f32[4,1326,1326]{2,1,0:T(8,128)}, f32[4,8]{1,0:T(4,128)S(1)}, /*index=5*/s32[]{:T(128)}) while((s32[]{:T(128)}, f32[4,8,1326]{2,1,0:T(8,128)S(1)}, f32[4,8,1326]{2,1,0:T(8,128)S(1)}, f32[4,1326,1326]{2,1,0:T(8,128)}, f32[4,8]{1,0:T(4,128)S(1)}, ...), condition=%wide.region_12.13_spmd, body=%wide.region_11.12_spmd.sunk | while | flops 168805120 | bytes 7571593 | solution.py:65
  164.6 9.0 %fusion.99 = f32[4,8,1326]{2,1,0:T(8,128)S(1)} fusion(f32[4,8,1326]{2,1,0:T(8,128)S(1)} %get-tuple-element.372, s32[]{:T(128)} %get-tuple-element.371, f32[4,1326,1326]{2,1,0:T(8,128)} %get-tuple-element.380, f32[4,8,1326]{2,1,0:T(8,128)S(1)} %get-tuple-element.379, f32[8]{0:T(128)S(1)} %fusion.98), kind=kOutput, calls=%fused_computation.25.clone.1 | convolution fusion | flops 168805104 | bytes 7571456 | tf_op jit(solution)/shard_map/while/body/eval_jaxpr/dot_general | solution.py:62
  173.7 9.0 %fusion.99 = f32[4,8,1326]{2,1,0:T(8,128)S(1)} fusion(f32[4,8,1326]{2,1,0:T(8,128)S(1)} %get-tuple-element.372, s32[]{:T(128)} %get-tuple-element.371, f32[4,1326,1326]{2,1,0:T(8,128)} %get-tuple-element.380, f32[4,8,1326]{2,1,0:T(8,128)S(1)} %get-tuple-element.379, f32[8]{0:T(128)S(1)} %fusion.98), kind=kOutput, calls=%fused_computation.25.clone.1 | convolution fusion | flops 168805104 | bytes 7571456 | tf_op jit(solution)/shard_map/while/body/eval_jaxpr/dot_general | solution.py:62
  182.7 9.0 %fusion.99 = f32[4,8,1326]{2,1,0:T(8,128)S(1)} fusion(f32[4,8,1326]{2,1,0:T(8,128)S(1)} %get-tuple-element.372, s32[]{:T(128)} %get-tuple-element.371, f32[4,1326,1326]{2,1,0:T(8,128)} %get-tuple-element.380, f32[4,8,1326]{2,1,0:T(8,128)S(1)} %get-tuple-element.379, f32[8]{0:T(128)S(1)} %fusion.98), kind=kOutput, calls=%fused_computation.25.clone.1 | convolution fusion | flops 168805104 | bytes 7571456 | tf_op jit(solution)/shard_map/while/body/eval_jaxpr/dot_general | solution.py:62
  191.7 9.0 %fusion.99 = f32[4,8,1326]{2,1,0:T(8,128)S(1)} fusion(f32[4,8,1326]{2,1,0:T(8,128)S(1)} %get-tuple-element.372, s32[]{:T(128)} %get-tuple-element.371, f32[4,1326,1326]{2,1,0:T(8,128)} %get-tuple-element.380, f32[4,8,1326]{2,1,0:T(8,128)S(1)} %get-tuple-element.379, f32[8]{0:T(128)S(1)} %fusion.98), kind=kOutput, calls=%fused_computation.25.clone.1 | convolution fusion | flops 168805104 | bytes 7571456 | tf_op jit(solution)/shard_map/while/body/eval_jaxpr/dot_general | solution.py:62
  200.7 0.9 scatter_custom_fusion.3
  201.7 4.8 %collective-permute-start.8 = (f32[1,1326]{1,0:T(1,128)S(1)}, f32[1,1326]{1,0:T(1,128)S(1)}, u32[]{:S(2)}, u32[]{:S(2)}) collective-permute-start(f32[1,1326]{1,0:T(1,128)S(1)} %constant_dynamic-slice_fusion.2), channel_id=1, source_target_pairs={{0,2},{2,4},{4,6},{6,8},{8,10},{10,12},{12,14},{14,16},{16,18},{18... | collective-permute-start | bytes 15920 | tf_op jit(solution)/shard_map/ppermute | solution.py:21
  206.5 1.3 collective-permute-done.8
  207.9 1.3 collective-permute-start.9
  209.3 4.3 %collective-permute-done.9 = f32[1,1326]{1,0:T(1,128)S(1)} collective-permute-done((f32[1,1326]{1,0:T(1,128)S(1)}, f32[1,1326]{1,0:T(1,128)S(1)}, u32[]{:S(2)}, u32[]{:S(2)}) %collective-permute-start.9) | collective-permute-done | bytes 5336 | tf_op jit(solution)/shard_map/ppermute | solution.py:22
  215.7 40.1 %psum.15 = f32[]{:T(128)} all-reduce(f32[]{:T(128)} %fusion.47), channel_id=1, replica_groups=mesh['leaf'=16,'player'=2] {'leaf'}, use_global_device_ids=true, to_apply=%region_15.16 | all-reduce | flops 1 | bytes 8 | tf_op jit(solution)/shard_map/psum | solution.py:108
  256.5 0.7 fusion.49
  (63 shorter events, 10.6 us)
Async XLA Ops:
  7.4 14.2 %collective-permute-start = (f32[1,1326]{1,0:T(1,128)S(1)}, f32[1,1326]{1,0:T(1,128)S(1)}, u32[]{:S(2)}, u32[]{:S(2)}) collective-permute-start(f32[1,1326]{1,0:T(1,128)S(1)} %constant_dynamic-slice_fusion.6), channel_id=1, source_target_pairs={{0,2},{2,4},{4,6},{6,8},{8,10},{10,12},{12,14},{14,16},{16,18},{18... | collective-permute-start | bytes 15920 | tf_op jit(solution)/shard_map/ppermute | solution.py:21
  14.0 5.1 %copy-start.5 = (s32[2]{0:T(128)S(1)}, s32[2]{0:T(128)}, u32[]{:S(2)}) copy-start(s32[2]{0:T(128)} %constant.243.clone.1) | copy-start | bytes 28
  14.0 5.8 %copy-start.3 = (s32[1,512]{1,0:T(1,128)S(1)}, s32[1,512]{1,0:T(1,128)}, u32[]{:S(2)}) copy-start(s32[1,512]{1,0:T(1,128)} %param.32) | copy-start | bytes 6148
  14.0 14.6 %copy-start = (f32[1,32,1326]{2,1,0:T(8,128)S(1)}, f32[1,32,1326]{2,1,0:T(8,128)}, u32[]{:S(2)}) copy-start(f32[1,32,1326]{2,1,0:T(8,128)} %param.30) | copy-start | bytes 509188
  14.0 14.6 %copy-start.2 = (f32[1,32,1326]{2,1,0:T(8,128)S(1)}, f32[1,32,1326]{2,1,0:T(8,128)}, u32[]{:S(2)}) copy-start(f32[1,32,1326]{2,1,0:T(8,128)} %param.29) | copy-start | bytes 509188
  21.7 5.5 %collective-permute-start.1 = (f32[1,1326]{1,0:T(1,128)S(1)}, f32[1,1326]{1,0:T(1,128)S(1)}, u32[]{:S(2)}, u32[]{:S(2)}) collective-permute-start(f32[1,1326]{1,0:T(1,128)S(1)} %get-tuple-element.226), channel_id=1, source_target_pairs={{2,0},{4,2},{6,4},{8,6},{10,8},{12,10},{14,12},{16,14},{18,16},{20... | collective-permute-start | bytes 15920 | tf_op jit(solution)/shard_map/ppermute | solution.py:22
  28.6 30.8 %collective-permute-start.2 = (f32[32,1326]{1,0:T(8,128)S(1)}, f32[32,1326]{1,0:T(8,128)S(1)}, u32[]{:S(2)}, u32[]{:S(2)}) collective-permute-start(f32[32,1326]{1,0:T(8,128)S(1)} %bitcast_multiply_fusion.6), channel_id=1, source_target_pairs={{0,1},{1,0},{2,3},{3,2},{4,5},{5,4},{6,7},{7,6},{8,9},{9,8},{10,11... | collective-permute-start | bytes 509192 | tf_op jit(solution)/shard_map/ppermute | solution.py:28
  28.7 30.6 %copy-start.4 = (f32[32]{0:T(128)S(1)}, f32[32]{0:T(128)}, u32[]{:S(2)}) copy-start(f32[32]{0:T(128)} %param.31) | copy-start | bytes 388
  96.5 5.6 %collective-permute-start.3 = (f32[1,1326]{1,0:T(1,128)S(1)}, f32[1,1326]{1,0:T(1,128)S(1)}, u32[]{:S(2)}, u32[]{:S(2)}) collective-permute-start(f32[1,1326]{1,0:T(1,128)S(1)} %constant_dynamic-slice_fusion.4), channel_id=1, source_target_pairs={{0,2},{2,4},{4,6},{6,8},{8,10},{10,12},{12,14},{14,16},{16,18},{18... | collective-permute-start | bytes 15920 | tf_op jit(solution)/shard_map/ppermute | solution.py:21
  102.1 5.8 %collective-permute-start.4 = (f32[1,1326]{1,0:T(1,128)S(1)}, f32[1,1326]{1,0:T(1,128)S(1)}, u32[]{:S(2)}, u32[]{:S(2)}) collective-permute-start(f32[1,1326]{1,0:T(1,128)S(1)} %get-tuple-element.224), channel_id=1, source_target_pairs={{2,0},{4,2},{6,4},{8,6},{10,8},{12,10},{14,12},{16,14},{18,16},{20... | collective-permute-start | bytes 15920 | tf_op jit(solution)/shard_map/ppermute | solution.py:22
  153.1 2.6 %collective-permute-start.5 = (f32[1,1326]{1,0:T(1,128)S(1)}, f32[1,1326]{1,0:T(1,128)S(1)}, u32[]{:S(2)}, u32[]{:S(2)}) collective-permute-start(f32[1,1326]{1,0:T(1,128)S(1)} %constant_dynamic-slice_fusion.3), channel_id=1, source_target_pairs={{0,2},{2,4},{4,6},{6,8},{8,10},{10,12},{12,14},{14,16},{16,18},{18... | collective-permute-start | bytes 15920 | tf_op jit(solution)/shard_map/ppermute | solution.py:21
  155.7 5.8 %collective-permute-start.6 = (f32[1,1326]{1,0:T(1,128)S(1)}, f32[1,1326]{1,0:T(1,128)S(1)}, u32[]{:S(2)}, u32[]{:S(2)}) collective-permute-start(f32[1,1326]{1,0:T(1,128)S(1)} %get-tuple-element.222), channel_id=1, source_target_pairs={{2,0},{4,2},{6,4},{8,6},{10,8},{12,10},{14,12},{16,14},{18,16},{20... | collective-permute-start | bytes 15920 | tf_op jit(solution)/shard_map/ppermute | solution.py:22
  163.1 1.5 collective-permute-start.7
  200.7 56.5 %copy-start.1 = (f32[4,8,1326]{2,1,0:T(8,128)}, f32[4,8,1326]{2,1,0:T(8,128)S(1)}, u32[]{:S(2)}) copy-start(f32[4,8,1326]{2,1,0:T(8,128)S(1)} %get-tuple-element.181) | copy-start | bytes 509188
  201.7 6.1 %collective-permute-start.8 = (f32[1,1326]{1,0:T(1,128)S(1)}, f32[1,1326]{1,0:T(1,128)S(1)}, u32[]{:S(2)}, u32[]{:S(2)}) collective-permute-start(f32[1,1326]{1,0:T(1,128)S(1)} %constant_dynamic-slice_fusion.2), channel_id=1, source_target_pairs={{0,2},{2,4},{4,6},{6,8},{8,10},{10,12},{12,14},{14,16},{16,18},{18... | collective-permute-start | bytes 15920 | tf_op jit(solution)/shard_map/ppermute | solution.py:21
  207.9 5.8 %collective-permute-start.9 = (f32[1,1326]{1,0:T(1,128)S(1)}, f32[1,1326]{1,0:T(1,128)S(1)}, u32[]{:S(2)}, u32[]{:S(2)}) collective-permute-start(f32[1,1326]{1,0:T(1,128)S(1)} %get-tuple-element.220), channel_id=1, source_target_pairs={{2,0},{4,2},{6,4},{8,6},{10,8},{12,10},{14,12},{16,14},{18,16},{20... | collective-permute-start | bytes 15920 | tf_op jit(solution)/shard_map/ppermute | solution.py:22
where the time goes:
time: 258 us; the launch traced here: 257 us
  blocking collectives  81.5 us (32%)
  matrix products  76.9 us (30%)
  other arithmetic  41.5 us (16%)
  waiting for transfers between devices  21.1 us (8%)
  starting transfers between devices  20.6 us (8%)
  local copies, waits for them, and re-layouts  8.31 us (3%)
  between operations  7.02 us (3%)
    psum x2, blocking collectives, local(): squares = lax.psum(jnp.sum(instant * instant), 'leaf')  81.5 us
    dot_general x8, matrix products, one_board(): summed = jnp.dot(opp_block, matrix.T, precision=lax.Precision.HIGHEST)  71.9 us
    dynamic_update_slice x4, other arithmetic, local(): lax.map(lambda items: payoff_matrix(items[0], items[1], apart_mask), (han...  27.5 us
    ppermute x4, waiting for transfers between devices, extended(): after = lax.ppermute(first, axis, down)  15.7 us
    ppermute x4, starting transfers between devices, extended(): before = lax.ppermute(last, axis, up)  15.3 us
    ppermute x4, starting transfers between devices, extended(): after = lax.ppermute(first, axis, down)  5.17 us
  transfers between devices with their start and end apart: 10, of which 8 were waited for; matrix products, arithmetic and copies ran while one was open for 15% of the time, Pallas kernels for 0%

commit v1 on v0

v1 whole, which is shorter than its diff:
```python
import functools

import jax
import jax.numpy as jnp
from jax import lax
from jax.experimental import pallas as pl
from jax.experimental.pallas import tpu as pltpu
from jax.sharding import PartitionSpec as P

ITERS = 2
DELTA = 0.05
EPSILON = 1e-06
DECK_SIZE = 52
LANES = 128
WIDE = 256
SPLIT = 5
MESH = pl.DeviceIdType.MESH
HIGHEST = lax.Precision.HIGHEST
F32 = jnp.float32
BF16 = jnp.bfloat16


def round_up(value, unit):
    return (value + unit - 1) // unit * unit


def column_of(row, count):
    down = lax.broadcasted_iota(jnp.int32, (count, count), 0)
    across = lax.broadcasted_iota(jnp.int32, (count, count), 1)
    return jnp.sum(jnp.where(down == across, row, 0.0), axis=1, keepdims=True)


def row_of(column, count):
    down = lax.broadcasted_iota(jnp.int32, (count, count), 0)
    across = lax.broadcasted_iota(jnp.int32, (count, count), 1)
    return jnp.sum(jnp.where(down == across, column, 0.0), axis=0, keepdims=True)


def kernel(
    n, boards, rows, hands, leaf_count,
    chance, regrets, pot, parent, cards, board_cards, rank,
    out_regrets, out_values,
    payoff, left, right, high, free, cards_wide, rank_wide, pots, same, split,
    held, policy, reach, opposed, values, square_out, square_in,
    held_send, held_recv, value_send, value_recv, reach_send, reach_recv, square_send, square_recv,
):
    me = lax.axis_index("leaf")
    player = lax.axis_index("player")
    before, after = lax.rem(me + n - 1, n), lax.rem(me + 1, n)
    width = payoff.shape[1]
    depth = left.shape[0]
    chunks = boards + 2
    total = chunks * rows

    zeros = jnp.zeros((rows, hands), F32)
    for edge in (0, chunks - 1):
        held[edge] = zeros
        for it in range(ITERS):
            values[it, edge] = zeros

    barrier = pltpu.get_barrier_semaphore()

    def greet(k, carry):
        pl.semaphore_signal(barrier, inc=1, device_id={"leaf": lax.rem(me + k, n)}, device_id_type=MESH)
        return carry

    pl.semaphore_signal(barrier, inc=1, device_id={"player": 1 - player}, device_id_type=MESH)
    lax.fori_loop(1, n, greet, 0)

    cards_wide[...] = jnp.full(cards_wide.shape, -1, jnp.int32)
    cards_wide[:, :hands] = cards[...]
    rank_wide[...] = jnp.zeros(rank_wide.shape, jnp.int32)
    rank_wide[:boards, :hands] = rank[...]
    card = lax.broadcasted_iota(jnp.int32, (depth, width), 0)
    lane = lax.broadcasted_iota(jnp.int32, (depth, width), 1)
    holding = ((card == cards_wide[0:1, :]) | (card == cards_wide[1:2, :])).astype(F32)
    valid = ((card == depth - 1) & (lane < hands)).astype(F32)
    ranked = rank_wide[...]
    code = ((128 + (ranked & 127)) << (ranked >> 7)).astype(F32)
    left[...] = holding + valid
    left[DECK_SIZE : DECK_SIZE + boards, :] = code[:boards]
    right[:, :width] = (valid - holding).astype(BF16)
    pick = lax.broadcasted_iota(jnp.int32, (depth, boards * LANES), 0) - DECK_SIZE
    spot = lax.broadcasted_iota(jnp.int32, (depth, boards * LANES), 1)
    right[:, width:] = ((spot >= pick * LANES) & (spot < pick * LANES + LANES)).astype(BF16)
    for b in range(boards):
        high[b] = jnp.broadcast_to(code[b : b + 1], (16, width)).astype(BF16)
    deck = lax.broadcasted_iota(jnp.int32, (boards, depth), 1)
    on_board = jnp.zeros((boards, depth), jnp.bool_)
    for k in range(board_cards.shape[1]):
        on_board = on_board | (deck == board_cards[:, k : k + 1])
    touched = jnp.dot(on_board.astype(BF16), holding.astype(BF16), preferred_element_type=F32)
    free[...] = (touched < 0.5).astype(F32)

    def build(i, carry):
        start = pl.multiple_of(i * LANES, LANES)
        down = left[:, pl.ds(start, LANES)].T.astype(BF16)
        lows = jnp.dot(down, right[:, width:], preferred_element_type=F32).astype(BF16)
        for first in range(0, width, WIDE):
            last = min(first + WIDE, width)
            apart = jnp.dot(down, right[:, first:last], preferred_element_type=F32)
            apart = jnp.maximum(apart, 0.0).astype(BF16)
            for at in range(first, last, LANES):
                bound = apart[:, at - first : at - first + LANES].reshape(LANES // 16, 16, LANES)
                for b in range(boards):
                    low = lows[:, b * LANES : (b + 1) * LANES].reshape(LANES // 16, 16, LANES)
                    gap = high[b, :, at : at + LANES][None] - low
                    entry = jnp.minimum(jnp.maximum(gap, -bound), bound)
                    payoff[b, pl.ds(start, LANES), at : at + LANES] = entry.reshape(LANES, LANES)
        return carry

    blocks = width // LANES
    lax.fori_loop(0, SPLIT, build, 0)

    pl.semaphore_wait(barrier, n)

    def to_before(source, target, send, recv):
        return pltpu.make_async_remote_copy(
            src_ref=source, dst_ref=target, send_sem=send, recv_sem=recv,
            device_id={"leaf": before}, device_id_type=MESH)

    def to_after(source, target, send, recv):
        return pltpu.make_async_remote_copy(
            src_ref=source, dst_ref=target, send_sem=send, recv_sem=recv,
            device_id={"leaf": after}, device_id_type=MESH)

    held_down = to_before(regrets.at[0, pl.ds(0, rows)], held.at[chunks - 1], held_send.at[0], held_recv.at[0])
    held_up = to_after(
        regrets.at[0, pl.ds((boards - 1) * rows, rows)], held.at[0], held_send.at[1], held_recv.at[1])
    value_down = [
        to_before(values.at[it, 1], values.at[it, chunks - 1], value_send.at[it, 0], value_recv.at[it, 0])
        for it in range(ITERS)]
    value_up = [
        to_after(values.at[it, boards], values.at[it, 0], value_send.at[it, 1], value_recv.at[it, 1])
        for it in range(ITERS)]

    @pl.when(me > 0)
    def _():
        held_down.start()

    @pl.when(me < n - 1)
    def _():
        held_up.start()

    leaf = me * (boards * rows) - rows + lax.broadcasted_iota(jnp.int32, (total, leaf_count), 0)
    here = lax.broadcasted_iota(jnp.int32, (total, leaf_count), 1)
    ids = jnp.sum(jnp.where(leaf == here, parent[...].astype(F32) + 1.0, 0.0), axis=1, keepdims=True)
    same[...] = (ids == row_of(ids, total)).astype(F32)
    pots[...] = jnp.broadcast_to(
        column_of(pot[...], boards * rows) * (1.0 / hands), (boards * rows, LANES)).reshape(boards, rows, LANES)
    split[...] = jnp.zeros(split.shape, BF16)
    for b in range(boards):
        held[b + 1] = regrets[0, pl.ds(b * rows, rows)]

    lax.fori_loop(SPLIT, blocks, build, 0)

    def node_totals(array):
        return jnp.dot(same[...], array, precision=HIGHEST, preferred_element_type=F32)

    @pl.when(me > 0)
    def _():
        held_up.wait_recv()

    @pl.when(me < n - 1)
    def _():
        held_down.wait_recv()

    standing = held[...].reshape(total, hands)
    for it in range(ITERS):
        positive = jnp.maximum(standing, 0.0) + DELTA
        policy[it] = positive / node_totals(positive)
        own_policy = policy[it, rows : rows + boards * rows]
        reach[it] = (chance[0] * own_policy).reshape(boards, rows, hands)

        def exchange(b, it=it):
            return pltpu.make_async_remote_copy(
                src_ref=reach.at[it, b], dst_ref=opposed.at[it, b],
                send_sem=reach_send.at[it, b], recv_sem=reach_recv.at[it, b],
                device_id={"player": 1 - player}, device_id_type=MESH)

        for t in range(boards):
            exchange(t * (boards - 1) % boards).start()

        def showdown(t, carry, it=it, exchange=exchange):
            b = lax.rem(t * (boards - 1), boards)
            exchange(b).wait_recv()
            open_hands = free[pl.ds(b, 1), :]
            facing = opposed[it, b] * open_hands[:, :hands]
            coarse = facing.astype(BF16).astype(F32)
            split[:, :hands] = jnp.concatenate([coarse, facing - coarse], axis=0).astype(BF16)
            summed = jnp.dot(split[...], payoff[b], preferred_element_type=F32)
            summed = (summed[:rows] + summed[rows:]) * open_hands * pots[b][:, :1]
            values[it, b + 1] = summed[:, :hands]

            @pl.when((t == 0) & (me > 0))
            def _():
                value_down[it].start()

            @pl.when((t == 1) & (me < n - 1))
            def _():
                value_up[it].start()

            return carry

        lax.fori_loop(0, boards, showdown, 0)

        @pl.when(me > 0)
        def _(it=it):
            value_up[it].wait_recv()

        @pl.when(me < n - 1)
        def _(it=it):
            value_down[it].wait_recv()

        gained = values[it].reshape(total, hands)
        instant = gained - node_totals(policy[it] * gained)
        own = instant[rows : rows + boards * rows]
        squares = jnp.sum(jnp.sum(own * own, axis=0, keepdims=True), axis=1, keepdims=True)
        square_out[it] = jnp.broadcast_to(squares, (1, LANES))

        def tell(k, carry, it=it):
            pltpu.make_async_remote_copy(
                src_ref=square_out.at[it], dst_ref=square_in.at[it, k - 1],
                send_sem=square_send.at[it], recv_sem=square_recv.at[it],
                device_id={"leaf": lax.rem(me + k, n)}, device_id_type=MESH).start()
            return carry

        lax.fori_loop(1, n, tell, 0)
        if it == ITERS - 1:
            out_values[0] = gained[rows : rows + boards * rows]
        everyone = square_in.at[it]
        pltpu.make_async_copy(everyone, everyone, square_recv.at[it]).wait()
        squares = square_out[it] + jnp.sum(square_in[it], axis=0)
        inverse = 1.0 / jnp.sqrt(squares[:, :1] / (leaf_count * hands) + EPSILON)
        if it < ITERS - 1:
            standing = standing + instant * inverse
        else:
            out_regrets[0] = standing[rows : rows + boards * rows] + own * inverse

    @pl.when(me > 0)
    def _():
        held_down.wait_send()
        for it in range(ITERS):
            value_down[it].wait_send()

    @pl.when(me < n - 1)
    def _():
        held_up.wait_send()
        for it in range(ITERS):
            value_up[it].wait_send()

    for it in range(ITERS):
        everyone = square_in.at[it]
        pltpu.make_async_copy(everyone, everyone, square_send.at[it]).wait()
        for b in range(boards):
            pltpu.make_async_copy(reach.at[it, b], reach.at[it, b], reach_send.at[it, b]).wait()


def solution(mesh):
    n = mesh.shape["leaf"]

    def local(chance_reach, regrets_start, pot, parent, hand_cards, board_cards, hand_rank):
        leaf_rows, hands = chance_reach.shape[1:]
        boards = hand_rank.shape[0]
        rows = leaf_rows // boards
        leaf_count = parent.shape[1]
        width = round_up(hands, LANES)
        depth = round_up(DECK_SIZE + boards + 1, 16)
        chunks = boards + 2
        vmem = pl.BlockSpec(memory_space=pltpu.VMEM)
        shape = jax.ShapeDtypeStruct(chance_reach.shape, F32)
        dma = pltpu.SemaphoreType.DMA
        return pl.pallas_call(
            functools.partial(kernel, n, boards, rows, hands, leaf_count),
            out_shape=(shape, shape),
            in_specs=[vmem] * 7,
            out_specs=(vmem, vmem),
            scratch_shapes=[
                pltpu.VMEM((boards, width, width), BF16),
                pltpu.VMEM((depth, width), F32),
                pltpu.VMEM((depth, width + boards * LANES), BF16),
                pltpu.VMEM((boards, 16, width), BF16),
                pltpu.VMEM((boards, width), F32),
                pltpu.VMEM((2, width), jnp.int32),
                pltpu.VMEM((round_up(boards, 8), width), jnp.int32),
                pltpu.VMEM((boards, rows, LANES), F32),
                pltpu.VMEM((chunks * rows, chunks * rows), F32),
                pltpu.VMEM((2 * rows, width), BF16),
                pltpu.VMEM((chunks, rows, hands), F32),
                pltpu.VMEM((ITERS, chunks * rows, hands), F32),
                pltpu.VMEM((ITERS, boards, rows, hands), F32),
                pltpu.VMEM((ITERS, boards, rows, hands), F32),
                pltpu.VMEM((ITERS, chunks, rows, hands), F32),
                pltpu.VMEM((ITERS, 1, LANES), F32),
                pltpu.VMEM((ITERS, n - 1, 1, LANES), F32),
                dma((2,)), dma((2,)),
                dma((ITERS, 2)), dma((ITERS, 2)),
                dma((ITERS, boards)), dma((ITERS, boards)),
                dma((ITERS,)), dma((ITERS,)),
            ],
            compiler_params=pltpu.CompilerParams(collective_id=0, has_side_effects=True),
            name="regret",
        )(chance_reach, regrets_start, pot[None], parent, hand_cards.T, board_cards, hand_rank)

    in_specs = (
        P("player", "leaf", None),
        P("player", "leaf", None),
        P("leaf"),
        P("player", None),
        P(),
        P("leaf", None),
        P("leaf", None),
    )
    out_specs = (P("player", "leaf", None), P("player", "leaf", None))
    return jax.shard_map(local, mesh=mesh, in_specs=in_specs, out_specs=out_specs, check_vma=False)
```

time: 258 us -> 37.1 us (0.14)
  blocking collectives: 81.5 us -> 0 us
  matrix products: 76.9 us -> 0 us
  other arithmetic: 41.5 us -> 0 us
  Pallas kernels: 0 us -> 34 us
  waiting for transfers between devices: 21.1 us -> 0 us
  starting transfers between devices: 20.6 us -> 0 us
  between operations: 7.02 us -> 0.65 us
  local copies, waits for them, and re-layouts: 8.31 us -> 2.32 us
    psum x2 -> x0, blocking collectives: 81.5 us -> none  [local(): squares = lax.psum(jnp.sum(instant * instant), 'leaf')]
    dot_general x10 -> x0, matrix products: 76.9 us -> none  [the longest x8 71.9 us: one_board(): summed = jnp.dot(opp_block, matrix.T, precision=lax.Precision.HIGHEST)]
    pallas_call x0 -> x1, Pallas kernels: none -> 34 us  [local(): pl.pallas_call(functools.partial(kernel, n, boards, rows, hands, leaf_cou...]
    dynamic_update_slice x4 -> x0, other arithmetic: 27.5 us -> none  [local(): lax.map(lambda items: payoff_matrix(items[0], items[1], apart_mask), (han...]
    ppermute x10 -> x0, waiting for transfers between devices: 21.1 us -> none  [the longest x4 15.7 us: extended(): after = lax.ppermute(first, axis, down)]
    ppermute x10 -> x0, starting transfers between devices: 20.6 us -> none  [the longest x4 15.3 us: extended(): before = lax.ppermute(last, axis, up)]
    scatter-add x4 -> x0, other arithmetic: 4.16 us -> none  [node_totals(): jax.ops.segment_sum(values, local_ids, num_segments=leaf_rows)]
    another operation x9 -> x0, other arithmetic: 3.11 us -> none
  transfers between devices with their start and end apart: 10 -> 0, of which waited for: 8 -> 0; matrix products, arithmetic and copies ran while one was open for 15% -> 0% of each run, Pallas kernels for 0% -> 0%
where the time goes in v1:
time: 37.1 us; the launch traced here: 36.9 us
  Pallas kernels  34 us (92%)
  local copies, waits for them, and re-layouts  2.32 us (6%)
  between operations  0.65 us (2%)
    pallas_call x1, Pallas kernels, local(): pl.pallas_call(functools.partial(kernel, n, boards, rows, hands, leaf_cou...  34 us
    unnamed x4, local copies, waits for them, and re-layouts  2.32 us

profile of v1, /device:TPU:0, one launch (start us, length us, event | category | flops | bytes accessed | tf_op | source)
XLA Modules:
  0.0 36.9 jit_solution(8908676146424508471)
XLA Ops:
  0.6 34.0 %regret.1 = (f32[1,32,1326]{2,1,0:T(8,128)}, f32[1,32,1326]{2,1,0:T(8,128)}) custom-call(f32[1,32,1326]{2,1,0:T(8,128)} %chance.1, f32[1,32,1326]{2,1,0:T(8,128)} %regrets.1, f32[1,32]{1,0:T(1,128)} %bitcast.3, s32[1,512]{1,0:T(1,128)} %parent.1, s32[2,1326]{1,0:T(2,128)} %bitcast.2, s32[4,5]{1,0:T(4,128)} %board_cards.1, s32[4,1326]{1,0:T(4,128)} %rank.1), custom_call_target="tpu_custom_call" | custom-call | tf_op jit(solution)/shard_map/regret/pallas_call | solution.py:273
  34.6 0.0 copy-start
  34.6 1.6 %copy.11 = f32[1,32,1326]{2,1,0:T(8,128)} copy(f32[1,32,1326]{2,1,0:T(8,128)} %get-tuple-element.4) | data formatting | bytes 339456
  36.3 0.0 copy-done
  36.3 0.7 %copy.12 = f32[1,32,1326]{2,1,0:T(8,128)} copy(f32[1,32,1326]{2,1,0:T(8,128)S(1)} %copy-done) | data formatting | bytes 339456
Async XLA Ops:
  34.6 1.7 %copy-start = (f32[1,32,1326]{2,1,0:T(8,128)S(1)}, f32[1,32,1326]{2,1,0:T(8,128)}, u32[]{:S(2)}) copy-start(f32[1,32,1326]{2,1,0:T(8,128)} %get-tuple-element.5) | copy-start | bytes 509188

commit v2 on v1

--- a/solution.py
+++ b/solution.py
@@ -15,7 +15,6 @@
 WIDE = 256
 SPLIT = 5
 MESH = pl.DeviceIdType.MESH
-HIGHEST = lax.Precision.HIGHEST
 F32 = jnp.float32
 BF16 = jnp.bfloat16
 
@@ -38,9 +37,10 @@
 
 def kernel(
     n, boards, rows, hands, leaf_count,
-    chance, regrets, pot, parent, cards, board_cards, rank,
+    chance_far, regrets_far, pot_far, parent_far, cards_far, board_cards_far, rank_far,
     out_regrets, out_values,
-    payoff, left, right, high, free, cards_wide, rank_wide, pots, same, split,
+    chance, regrets, pot, parent, cards, board_cards, rank, load,
+    payoff, left, right, high, lows, free, cards_wide, rank_wide, pots, same, split,
     held, policy, reach, opposed, values, square_out, square_in,
     held_send, held_recv, value_send, value_recv, reach_send, reach_recv, square_send, square_recv,
 ):
@@ -52,6 +52,14 @@
     chunks = boards + 2
     total = chunks * rows
 
+    loads = [
+        pltpu.make_async_copy(far, near, load.at[i])
+        for i, (far, near) in enumerate((
+            (cards_far, cards), (board_cards_far, board_cards), (rank_far, rank), (regrets_far, regrets),
+            (pot_far, pot), (parent_far, parent), (chance_far, chance)))]
+    for copy in loads:
+        copy.start()
+
     zeros = jnp.zeros((rows, hands), F32)
     for edge in (0, chunks - 1):
         held[edge] = zeros
@@ -66,6 +74,9 @@
 
     pl.semaphore_signal(barrier, inc=1, device_id={"player": 1 - player}, device_id_type=MESH)
     lax.fori_loop(1, n, greet, 0)
+
+    for copy in loads[:3]:
+        copy.wait()
 
     cards_wide[...] = jnp.full(cards_wide.shape, -1, jnp.int32)
     cards_wide[:, :hands] = cards[...]
@@ -95,23 +106,28 @@
     def build(i, carry):
         start = pl.multiple_of(i * LANES, LANES)
         down = left[:, pl.ds(start, LANES)].T.astype(BF16)
-        lows = jnp.dot(down, right[:, width:], preferred_element_type=F32).astype(BF16)
+        coded = jnp.dot(down, right[:, width:], preferred_element_type=F32).astype(BF16)
+        for b in range(boards):
+            lows[b] = coded[:, b * LANES : (b + 1) * LANES]
         for first in range(0, width, WIDE):
             last = min(first + WIDE, width)
             apart = jnp.dot(down, right[:, first:last], preferred_element_type=F32)
-            apart = jnp.maximum(apart, 0.0).astype(BF16)
+            apart = jnp.maximum(apart.astype(BF16), 0.0)
             for at in range(first, last, LANES):
-                bound = apart[:, at - first : at - first + LANES].reshape(LANES // 16, 16, LANES)
-                for b in range(boards):
-                    low = lows[:, b * LANES : (b + 1) * LANES].reshape(LANES // 16, 16, LANES)
-                    gap = high[b, :, at : at + LANES][None] - low
-                    entry = jnp.minimum(jnp.maximum(gap, -bound), bound)
-                    payoff[b, pl.ds(start, LANES), at : at + LANES] = entry.reshape(LANES, LANES)
+                for r in range(0, LANES, 16):
+                    bound = apart[r : r + 16, at - first : at - first + LANES]
+                    floor = -bound
+                    for b in range(boards):
+                        gap = high[b, :, at : at + LANES] - lows[b, r : r + 16]
+                        payoff[b, pl.ds(start + r, 16), at : at + LANES] = jnp.minimum(
+                            jnp.maximum(gap, floor), bound)
         return carry
 
     blocks = width // LANES
     lax.fori_loop(0, SPLIT, build, 0)
 
+    for copy in loads[3:]:
+        copy.wait()
     pl.semaphore_wait(barrier, n)
 
     def to_before(source, target, send, recv):
@@ -142,10 +158,11 @@
     def _():
         held_up.start()
 
-    leaf = me * (boards * rows) - rows + lax.broadcasted_iota(jnp.int32, (total, leaf_count), 0)
-    here = lax.broadcasted_iota(jnp.int32, (total, leaf_count), 1)
+    twice = lax.broadcasted_iota(jnp.int32, (2 * total, leaf_count), 0)
+    leaf = me * (boards * rows) - rows + jnp.where(twice >= total, twice - total, twice)
+    here = lax.broadcasted_iota(jnp.int32, (2 * total, leaf_count), 1)
     ids = jnp.sum(jnp.where(leaf == here, parent[...].astype(F32) + 1.0, 0.0), axis=1, keepdims=True)
-    same[...] = (ids == row_of(ids, total)).astype(F32)
+    same[...] = (ids[:total] == row_of(ids, 2 * total)).astype(BF16)
     pots[...] = jnp.broadcast_to(
         column_of(pot[...], boards * rows) * (1.0 / hands), (boards * rows, LANES)).reshape(boards, rows, LANES)
     split[...] = jnp.zeros(split.shape, BF16)
@@ -155,7 +172,9 @@
     lax.fori_loop(SPLIT, blocks, build, 0)
 
     def node_totals(array):
-        return jnp.dot(same[...], array, precision=HIGHEST, preferred_element_type=F32)
+        coarse = array.astype(BF16)
+        fine = (array - coarse.astype(F32)).astype(BF16)
+        return jnp.dot(same[...], jnp.concatenate([coarse, fine], axis=0), preferred_element_type=F32)
 
     @pl.when(me > 0)
     def _():
@@ -268,23 +287,27 @@
         depth = round_up(DECK_SIZE + boards + 1, 16)
         chunks = boards + 2
         vmem = pl.BlockSpec(memory_space=pltpu.VMEM)
-        shape = jax.ShapeDtypeStruct(chance_reach.shape, F32)
+        shape = pltpu.VMEM(chance_reach.shape, F32)
         dma = pltpu.SemaphoreType.DMA
+        arrays = (chance_reach, regrets_start, pot[None], parent, hand_cards.T, board_cards, hand_rank)
         return pl.pallas_call(
             functools.partial(kernel, n, boards, rows, hands, leaf_count),
             out_shape=(shape, shape),
-            in_specs=[vmem] * 7,
+            in_specs=[pl.BlockSpec(memory_space=pl.ANY)] * len(arrays),
             out_specs=(vmem, vmem),
             scratch_shapes=[
+                *(pltpu.VMEM(array.shape, array.dtype) for array in arrays),
+                pltpu.SemaphoreType.DMA((len(arrays),)),
                 pltpu.VMEM((boards, width, width), BF16),
                 pltpu.VMEM((depth, width), F32),
                 pltpu.VMEM((depth, width + boards * LANES), BF16),
                 pltpu.VMEM((boards, 16, width), BF16),
+                pltpu.VMEM((boards, LANES, LANES), BF16),
                 pltpu.VMEM((boards, width), F32),
                 pltpu.VMEM((2, width), jnp.int32),
                 pltpu.VMEM((round_up(boards, 8), width), jnp.int32),
                 pltpu.VMEM((boards, rows, LANES), F32),
-                pltpu.VMEM((chunks * rows, chunks * rows), F32),
+                pltpu.VMEM((chunks * rows, 2 * chunks * rows), BF16),
                 pltpu.VMEM((2 * rows, width), BF16),
                 pltpu.VMEM((chunks, rows, hands), F32),
                 pltpu.VMEM((ITERS, chunks * rows, hands), F32),
@@ -300,7 +323,7 @@
             ],
             compiler_params=pltpu.CompilerParams(collective_id=0, has_side_effects=True),
             name="regret",
-        )(chance_reach, regrets_start, pot[None], parent, hand_cards.T, board_cards, hand_rank)
+        )(*arrays)
 
     in_specs = (
         P("player", "leaf", None),

time: 37.1 us -> 35.5 us (0.957)
  local copies, waits for them, and re-layouts: 2.32 us -> 1.35 us
  Pallas kernels: 34 us -> 33.2 us
    unnamed x4 -> x2, local copies, waits for them, and re-layouts: 2.32 us -> 1.35 us
    pallas_call x1, Pallas kernels: 34 us -> 33.2 us  [local(): pl.pallas_call(functools.partial(kernel, n, boards, rows, hands, leaf_cou...]
where the time goes in v2:
time: 35.5 us; the launch traced here: 35.2 us
  Pallas kernels  33.2 us (94%)
  local copies, waits for them, and re-layouts  1.35 us (4%)
  between operations  0.64 us (2%)
    pallas_call x1, Pallas kernels, local(): pl.pallas_call(functools.partial(kernel, n, boards, rows, hands, leaf_cou...  33.2 us
    unnamed x2, local copies, waits for them, and re-layouts  1.35 us

profile of v2, /device:TPU:0, one launch (start us, length us, event | category | flops | bytes accessed | tf_op | source)
XLA Modules:
  0.0 35.2 jit_solution(17629168393251239155)
XLA Ops:
  0.6 33.2 %regret.1 = (f32[1,32,1326]{2,1,0:T(8,128)S(1)}, f32[1,32,1326]{2,1,0:T(8,128)S(1)}) custom-call(f32[1,32,1326]{2,1,0:T(8,128)} %chance_far.1, f32[1,32,1326]{2,1,0:T(8,128)} %regrets_far.1, f32[1,32]{1,0:T(1,128)} %bitcast.3, s32[1,512]{1,0:T(1,128)} %parent_far.1, s32[2,1326]{1,0:T(2,128)} %bitcast.2, s32[4,5]{1,0:T(4,128)} %board_cards_far.1, ...), custom_call_target="tpu_custom_call" | custom-call | tf_op jit(solution)/shard_map/regret/pallas_call | solution.py:293
  33.9 0.7 %copy.11 = f32[1,32,1326]{2,1,0:T(8,128)} copy(f32[1,32,1326]{2,1,0:T(8,128)S(1)} %get-tuple-element.2) | data formatting | bytes 339456
  34.6 0.7 %copy.12 = f32[1,32,1326]{2,1,0:T(8,128)} copy(f32[1,32,1326]{2,1,0:T(8,128)S(1)} %get-tuple-element.3) | data formatting | bytes 339456

commit v3 on v2

--- a/solution.py
+++ b/solution.py
@@ -8,6 +8,7 @@
 from jax.sharding import PartitionSpec as P
 
 ITERS = 2
+MOST = 6
 DELTA = 0.05
 EPSILON = 1e-06
 DECK_SIZE = 52
@@ -40,7 +41,7 @@
     chance_far, regrets_far, pot_far, parent_far, cards_far, board_cards_far, rank_far,
     out_regrets, out_values,
     chance, regrets, pot, parent, cards, board_cards, rank, load,
-    payoff, left, right, high, lows, free, cards_wide, rank_wide, pots, same, split,
+    payoff, left, right, free, cards_wide, rank_wide, pots, same, split,
     held, policy, reach, opposed, values, square_out, square_in,
     held_send, held_recv, value_send, value_recv, reach_send, reach_recv, square_send, square_recv,
 ):
@@ -94,8 +95,6 @@
     pick = lax.broadcasted_iota(jnp.int32, (depth, boards * LANES), 0) - DECK_SIZE
     spot = lax.broadcasted_iota(jnp.int32, (depth, boards * LANES), 1)
     right[:, width:] = ((spot >= pick * LANES) & (spot < pick * LANES + LANES)).astype(BF16)
-    for b in range(boards):
-        high[b] = jnp.broadcast_to(code[b : b + 1], (16, width)).astype(BF16)
     deck = lax.broadcasted_iota(jnp.int32, (boards, depth), 1)
     on_board = jnp.zeros((boards, depth), jnp.bool_)
     for k in range(board_cards.shape[1]):
@@ -106,19 +105,20 @@
     def build(i, carry):
         start = pl.multiple_of(i * LANES, LANES)
         down = left[:, pl.ds(start, LANES)].T.astype(BF16)
-        coded = jnp.dot(down, right[:, width:], preferred_element_type=F32).astype(BF16)
-        for b in range(boards):
-            lows[b] = coded[:, b * LANES : (b + 1) * LANES]
+        lows = jnp.dot(down, right[:, width:], preferred_element_type=F32).astype(BF16)
         for first in range(0, width, WIDE):
             last = min(first + WIDE, width)
             apart = jnp.dot(down, right[:, first:last], preferred_element_type=F32)
             apart = jnp.maximum(apart.astype(BF16), 0.0)
             for at in range(first, last, LANES):
+                highs = [
+                    jnp.broadcast_to(left[DECK_SIZE + b : DECK_SIZE + b + 1, at : at + LANES], (16, LANES)).astype(BF16)
+                    for b in range(boards)]
                 for r in range(0, LANES, 16):
                     bound = apart[r : r + 16, at - first : at - first + LANES]
                     floor = -bound
                     for b in range(boards):
-                        gap = high[b, :, at : at + LANES] - lows[b, r : r + 16]
+                        gap = highs[b] - lows[r : r + 16, b * LANES : (b + 1) * LANES]
                         payoff[b, pl.ds(start + r, 16), at : at + LANES] = jnp.minimum(
                             jnp.maximum(gap, floor), bound)
         return carry
@@ -140,14 +140,19 @@
             src_ref=source, dst_ref=target, send_sem=send, recv_sem=recv,
             device_id={"leaf": after}, device_id_type=MESH)
 
-    held_down = to_before(regrets.at[0, pl.ds(0, rows)], held.at[chunks - 1], held_send.at[0], held_recv.at[0])
+    reach_of = min(MOST - 1, rows)
+    held_down = to_before(
+        regrets.at[0, pl.ds(0, reach_of)], held.at[chunks - 1, pl.ds(0, reach_of)], held_send.at[0], held_recv.at[0])
     held_up = to_after(
-        regrets.at[0, pl.ds((boards - 1) * rows, rows)], held.at[0], held_send.at[1], held_recv.at[1])
+        regrets.at[0, pl.ds(boards * rows - reach_of, reach_of)], held.at[0, pl.ds(rows - reach_of, reach_of)], held_send.at[1], held_recv.at[1])
     value_down = [
-        to_before(values.at[it, 1], values.at[it, chunks - 1], value_send.at[it, 0], value_recv.at[it, 0])
+        to_before(
+            values.at[it, 1, pl.ds(0, reach_of)], values.at[it, chunks - 1, pl.ds(0, reach_of)], value_send.at[it, 0], value_recv.at[it, 0])
         for it in range(ITERS)]
     value_up = [
-        to_after(values.at[it, boards], values.at[it, 0], value_send.at[it, 1], value_recv.at[it, 1])
+        to_after(
+            values.at[it, boards, pl.ds(rows - reach_of, reach_of)], values.at[it, 0, pl.ds(rows - reach_of, reach_of)],
+            value_send.at[it, 1], value_recv.at[it, 1])
         for it in range(ITERS)]
 
     @pl.when(me > 0)
@@ -301,8 +306,6 @@
                 pltpu.VMEM((boards, width, width), BF16),
                 pltpu.VMEM((depth, width), F32),
                 pltpu.VMEM((depth, width + boards * LANES), BF16),
-                pltpu.VMEM((boards, 16, width), BF16),
-                pltpu.VMEM((boards, LANES, LANES), BF16),
                 pltpu.VMEM((boards, width), F32),
                 pltpu.VMEM((2, width), jnp.int32),
                 pltpu.VMEM((round_up(boards, 8), width), jnp.int32),

time: 35.5 us -> 33 us (0.930)
  Pallas kernels: 33.2 us -> 30.8 us
    pallas_call x1, Pallas kernels: 33.2 us -> 30.8 us  [local(): pl.pallas_call(functools.partial(kernel, n, boards, rows, hands, leaf_cou...]
where the time goes in v3:
time: 33 us; the launch traced here: 32.8 us
  Pallas kernels  30.8 us (93%)
  local copies, waits for them, and re-layouts  1.35 us (4%)
  between operations  0.64 us (2%)
    pallas_call x1, Pallas kernels, local(): pl.pallas_call(functools.partial(kernel, n, boards, rows, hands, leaf_cou...  30.8 us
    unnamed x2, local copies, waits for them, and re-layouts  1.35 us

profile of v3, /device:TPU:0, one launch (start us, length us, event | category | flops | bytes accessed | tf_op | source)
XLA Modules:
  0.0 32.8 jit_solution(10644122367460631349)
XLA Ops:
  0.6 30.8 %regret.1 = (f32[1,32,1326]{2,1,0:T(8,128)S(1)}, f32[1,32,1326]{2,1,0:T(8,128)S(1)}) custom-call(f32[1,32,1326]{2,1,0:T(8,128)} %chance_far.1, f32[1,32,1326]{2,1,0:T(8,128)} %regrets_far.1, f32[1,32]{1,0:T(1,128)} %bitcast.3, s32[1,512]{1,0:T(1,128)} %parent_far.1, s32[2,1326]{1,0:T(2,128)} %bitcast.2, s32[4,5]{1,0:T(4,128)} %board_cards_far.1, ...), custom_call_target="tpu_custom_call" | custom-call | tf_op jit(solution)/shard_map/regret/pallas_call | solution.py:298
  31.4 0.7 %copy.11 = f32[1,32,1326]{2,1,0:T(8,128)} copy(f32[1,32,1326]{2,1,0:T(8,128)S(1)} %get-tuple-element.2) | data formatting | bytes 339456
  32.1 0.7 %copy.12 = f32[1,32,1326]{2,1,0:T(8,128)} copy(f32[1,32,1326]{2,1,0:T(8,128)S(1)} %get-tuple-element.3) | data formatting | bytes 339456

commit v4 on v3

--- a/solution.py
+++ b/solution.py
@@ -14,7 +14,7 @@
 DECK_SIZE = 52
 LANES = 128
 WIDE = 256
-SPLIT = 5
+SPLIT = 3
 MESH = pl.DeviceIdType.MESH
 F32 = jnp.float32
 BF16 = jnp.bfloat16

time: 33 us -> 33.2 us (level)
  no operation moved by 1% of the time
where the time goes in v4:
time: 33.2 us; the launch traced here: 32.9 us
  Pallas kernels  30.9 us (93%)
  local copies, waits for them, and re-layouts  1.35 us (4%)
  between operations  0.64 us (2%)
    pallas_call x1, Pallas kernels, local(): pl.pallas_call(functools.partial(kernel, n, boards, rows, hands, leaf_cou...  30.9 us
    unnamed x2, local copies, waits for them, and re-layouts  1.35 us

profile of v4, /device:TPU:0, one launch (start us, length us, event | category | flops | bytes accessed | tf_op | source)
XLA Modules:
  0.0 32.9 jit_solution(8487229984648882361)
XLA Ops:
  0.6 30.9 %regret.1 = (f32[1,32,1326]{2,1,0:T(8,128)S(1)}, f32[1,32,1326]{2,1,0:T(8,128)S(1)}) custom-call(f32[1,32,1326]{2,1,0:T(8,128)} %chance_far.1, f32[1,32,1326]{2,1,0:T(8,128)} %regrets_far.1, f32[1,32]{1,0:T(1,128)} %bitcast.3, s32[1,512]{1,0:T(1,128)} %parent_far.1, s32[2,1326]{1,0:T(2,128)} %bitcast.2, s32[4,5]{1,0:T(4,128)} %board_cards_far.1, ...), custom_call_target="tpu_custom_call" | custom-call | tf_op jit(solution)/shard_map/regret/pallas_call | solution.py:298
  31.6 0.7 %copy.11 = f32[1,32,1326]{2,1,0:T(8,128)} copy(f32[1,32,1326]{2,1,0:T(8,128)S(1)} %get-tuple-element.2) | data formatting | bytes 339456
  32.3 0.7 %copy.12 = f32[1,32,1326]{2,1,0:T(8,128)} copy(f32[1,32,1326]{2,1,0:T(8,128)S(1)} %get-tuple-element.3) | data formatting | bytes 339456
